TPU v7x, 512 devices: a whole 4x8x8 slice. The times are simulated.
512 devices in a mesh: grp: 8 (over z), seq: 32 (over x, y_hi, core), hd: 2 (over y_lo).
Axes of the slice: x: 4, y: 8 (y_hi: 4, y_lo: 2; y = y_hi * 2 + y_lo), z: 8, core: 2. Of those that a mesh axis runs over, the one named last changes fastest.
Arguments:
- latent_qkv: bfloat16 [8, 32, 256, 3, 3072], P('grp', 'seq', None, None, 'hd'), may hold values from -6 to 6
- cross_query: bfloat16 [8, 32, 256, 3072], P('grp', 'seq', None, 'hd'), may hold values from -6 to 6
- residual: bfloat16 [8, 32, 256, 3072], P('grp', 'seq', None, 'hd'), may hold values from -4 to 4
- prompt_states: bfloat16 [8, 512, 4096], P(None, 'seq', 'grp'), may hold values from -6 to 6
- kv_weight: bfloat16 [4096, 2, 3072], P(('grp', 'seq'), None, 'hd'), may hold values from -0.09375 to 0.09375, as said below
- prompt_lengths: int32 [8], replicated, may hold values from 32 to 512
- assignment: int32 [8], replicated, may hold values from 0 to 7, each once
Outputs:
- block_out: bfloat16 [8, 32, 256, 3072], P('grp', 'seq', None, 'hd')
Inputs may be any that keep to these rules, and one draw needn't show every extreme that they name: Replica g serves prompt assignment[g]; every prompt is served by exactly one replica. `prompt_lengths`: key positions at or beyond a prompt's length are padding. `kv_weight`: entries have mean 0 and deviation 4096 ** -0.5.
All inputs are finite; a program needn't handle non-finite values.
Results may differ from a plain program's by a relative error of at most 0.0075.
Values may be sent and summed in bfloat16 or wider, within the bound.
A program may use at most 64 MiB of HBM per device.

v0:
```python
import math

import jax
import jax.numpy as jnp
from jax import lax
from jax.sharding import PartitionSpec as P

HDIM = 128


def attend(queries, key_rows, values, key_bias):
    scores = jnp.einsum("qhe,khe->hqk", queries, key_rows, preferred_element_type=jnp.float32)
    scores = scores / math.sqrt(queries.shape[-1]) + key_bias
    row_max = jnp.max(scores, axis=-1, keepdims=True)
    powered = jnp.exp(scores - row_max)
    weights = (powered / jnp.sum(powered, axis=-1, keepdims=True)).astype(jnp.bfloat16)
    return jnp.einsum("hqk,khe->qhe", weights, values, preferred_element_type=jnp.float32)


def frame_attention(mixed):
    frame_count, positions = (mixed.shape[0], mixed.shape[2])
    feat_width = mixed.shape[4]
    shaped = mixed.reshape(frame_count, positions, 3, feat_width // HDIM, HDIM)
    scores = jnp.einsum(
        "fnhe,gnhe->nhfg", shaped[:, :, 0], shaped[:, :, 1], preferred_element_type=jnp.float32
    )
    scores = scores / math.sqrt(HDIM)
    row_max = jnp.max(scores, axis=-1, keepdims=True)
    powered = jnp.exp(scores - row_max)
    weights = (powered / jnp.sum(powered, axis=-1, keepdims=True)).astype(jnp.bfloat16)
    mixed_out = jnp.einsum(
        "nhfg,gnhe->fnhe", weights, shaped[:, :, 2], preferred_element_type=jnp.float32
    )
    return mixed_out.astype(jnp.bfloat16).reshape(frame_count, 1, positions, feat_width)


def body(latent_qkv, cross_query, residual, prompt_states, kv_weight, prompt_lengths, assignment):
    spatial = latent_qkv.shape[2]
    feat_width = latent_qkv.shape[4]
    heads_here = feat_width // HDIM
    seq_count = lax.axis_size("seq")
    group_index = lax.axis_index("grp")
    picked = jnp.take(prompt_states, assignment, axis=0)
    slot_count, rows_here, feat_count = picked.shape
    flat_prompt = picked.reshape(slot_count * rows_here, feat_count)
    local = latent_qkv[0, 0].reshape(spatial, 3, heads_here, HDIM)
    spatial_out = attend(local[:, 0], local[:, 1], local[:, 2], jnp.float32(0.0))
    blocked = latent_qkv[0].reshape(1, seq_count, spatial // seq_count, 3, feat_width)
    moved = frame_attention(lax.all_to_all(blocked, "seq", split_axis=1, concat_axis=0, tiled=True))
    returned = lax.all_to_all(moved, "seq", split_axis=0, concat_axis=1, tiled=True)
    spatial_out, returned = (spatial_out, returned.reshape(spatial, feat_width))
    weight_piece = lax.all_gather(kv_weight, "seq", axis=0, tiled=True)
    piece_rows = weight_piece.shape[0]
    flat_piece = weight_piece.reshape(piece_rows, 2 * feat_width)
    partial_sum = jnp.dot(flat_prompt, flat_piece, preferred_element_type=jnp.float32)
    summed = lax.psum_scatter(partial_sum, "grp", scatter_dimension=0, tiled=True)
    own_rows = summed.astype(jnp.bfloat16).reshape(rows_here, 2, feat_width)
    pairs = lax.all_gather(own_rows, "seq", axis=0, tiled=True)
    prompt_total = pairs.shape[0]
    served = jnp.take(assignment, group_index)
    length_here = jnp.take(prompt_lengths, served)
    key_bias = jnp.where(jnp.arange(prompt_total) < length_here, 0.0, -1000000000.0).astype(
        jnp.float32
    )
    shaped_pairs = pairs.reshape(prompt_total, 2, heads_here, HDIM)
    crossing = cross_query[0, 0].reshape(spatial, heads_here, HDIM)
    cross_out = attend(crossing, shaped_pairs[:, 0], shaped_pairs[:, 1], key_bias)
    total = residual[0, 0].astype(jnp.float32) + spatial_out.reshape(spatial, feat_width)
    total = total + returned.astype(jnp.float32) + cross_out.reshape(spatial, feat_width)
    return total.astype(jnp.bfloat16)[None, None]


def solution(mesh):
    return jax.shard_map(
        body,
        mesh=mesh,
        in_specs=(
            P("grp", "seq", None, None, "hd"),
            P("grp", "seq", None, "hd"),
            P("grp", "seq", None, "hd"),
            P(None, "seq", "grp"),
            P(("grp", "seq"), None, "hd"),
            P(),
            P(),
        ),
        out_specs=P("grp", "seq", None, "hd"),
        check_vma=False,
    )
```

profile of v0, /device:TPU:321, one launch (start us, length us, event | category | flops | bytes accessed | tf_op | source)
XLA Modules:
  0.0 257.1 jit_solution(5249822375379424232)
XLA Ops:
  6.5 0.7 all-gather.3.cloned.1.call-update
  7.3 0.7 compare_select_fusion
  8.5 0.7 compare_and_fusion
  9.3 64.8 %all-gather.3.cloned.1.call-done = bf16[512,2,1536]{2,1,0:T(2,128)(2,1)} async-done(((bf16[16,2,1536]{2,1,0:T(2,128)(2,1)}), bf16[512,2,1536]{2,1,0:T(2,128)(2,1)}) %all-gather.3.cloned.1.call-update) | async-done | bytes 3145744 | tf_op jit(solution)/shard_map/all_gather | solution.py:52
  74.1 2.6 %copy.78 = bf16[64,8,2,1536]{3,1,2,0:T(8,128)(2,1)S(1)} copy(bf16[64,8,2,1536]{3,2,1,0:T(2,128)(2,1)} %bitcast.91) | data formatting | bytes 6291456
  76.8 1.8 fusion.32
  78.6 34.9 %reduce-scatter.2.cloned.1.call-done = f32[16,3072]{1,0:T(8,128)} async-done(((f32[128,3072]{1,0:T(8,128)}), f32[16,3072]{1,0:T(8,128)}) %reduce-scatter.2.cloned.1.call-update) | async-done | bytes 196624 | tf_op jit(solution)/shard_map/reduce_scatter | solution.py:56
  113.5 0.9 convert_element_type.46
  114.4 0.7 reshape.99
  115.1 1.6 copy.55
  116.7 14.7 %all-to-all-start = ((bf16[1,32,8,3,1536]{4,2,3,0,1:T(8,128)(2,1)}), bf16[1,32,8,3,1536]{4,2,3,0,1:T(8,128)(2,1)}, u32[]{:S(2)}, u32[]{:S(2)}) async-start(bf16[1,32,8,3,1536]{4,2,3,0,1:T(8,128)(2,1)} %copy.55), calls=%async_computation | async-start | bytes 4718592 | tf_op jit(solution)/shard_map/all_to_all | solution.py:49
  131.4 0.7 dynamic-slice.4
  132.8 2.5 copy.50
  135.9 1.2 copy.64
  137.1 2.0 fusion.21
  139.1 2.4 fusion.30
  141.5 1.6 fusion.18
  143.0 1.7 copy.54
  145.4 45.7 %all-to-all-done = bf16[1,32,8,3,1536]{4,2,3,0,1:T(8,128)(2,1)} async-done(((bf16[1,32,8,3,1536]{4,2,3,0,1:T(8,128)(2,1)}), bf16[1,32,8,3,1536]{4,2,3,0,1:T(8,128)(2,1)}, u32[]{:S(2)}, u32[]{:S(2)}) %all-to-all-start) | async-done | bytes 2359328 | tf_op jit(solution)/shard_map/all_to_all | solution.py:49
  191.0 4.2 %reshape.96 = bf16[32,8,3,12,128]{4,3,1,2,0:T(8,128)(2,1)S(1)} reshape(bf16[1,32,8,3,1536]{4,2,3,0,1:T(8,128)(2,1)} %all-to-all-done) | data formatting | bytes 4718592 | tf_op jit(solution)/shard_map/reshape | solution.py:23
  195.2 1.9 fusion.28
  197.1 3.3 %fusion.31 = (f32[8,12,32]{2,1,0:T(8,128)S(1)}, f32[8,12,32,32]{2,3,1,0:T(8,128)S(1)}) fusion(bf16[32,8,1,12,128]{4,3,1,2,0:T(8,128)(2,1)} %get-tuple-element.28, bf16[32,8,1,12,128]{4,3,1,2,0:T(8,128)(2,1)} %get-tuple-element.29), kind=kOutput, calls=%fused_computation.53 | convolution fusion | flops 25460768 | bytes 1978368 | tf_op jit(solution)/shard_map/sub | solution.py:29
  200.4 0.7 fusion.20
  201.1 1.4 copy.98
  202.5 6.7 %all-to-all-start.1 = ((bf16[32,1,8,1536]{3,2,1,0:T(8,128)(2,1)}), bf16[32,1,8,1536]{3,2,1,0:T(8,128)(2,1)}, u32[]{:S(2)}, u32[]{:S(2)}) async-start(bf16[32,1,8,1536]{3,2,1,0:T(8,128)(2,1)} %bitcast.83), calls=%async_computation.1 | async-start | bytes 1572864 | tf_op jit(solution)/shard_map/all_to_all | solution.py:50
  209.3 23.1 %all-gather.5.cloned.1.call-done = bf16[512,2,1536]{2,1,0:T(2,128)(2,1)} async-done(((bf16[16,2,1536]{2,1,0:T(2,128)(2,1)}), bf16[512,2,1536]{2,1,0:T(2,128)(2,1)}) %all-gather.5.cloned.1.call-update) | async-done | bytes 3145744 | tf_op jit(solution)/shard_map/all_gather | solution.py:58
  232.4 7.0 %copy.62 = bf16[512,2,1536]{0,2,1:T(8,128)(2,1)S(1)} copy(bf16[512,2,1536]{2,1,0:T(2,128)(2,1)} %all-gather.5.cloned.1.call-done) | data formatting | bytes 6291456 | tf_op jit(solution)/shard_map/all_gather | solution.py:58
  239.4 2.2 fusion.14
  241.6 2.5 fusion.29
  244.0 1.9 fusion.9
  245.9 2.0 copy.67
  247.9 2.7 %fusion.16 = bf16[1,1,256,1536]{3,2,1,0:T(8,128)(2,1)} fusion(f32[1,1,256,1536]{3,2,1,0:T(8,128)S(1)} %copy.67, f32[1,1,256,1536]{3,2,1,0:T(8,128)S(1)} %copy-done.2, bf16[1,1,256,1536]{3,2,1,0:T(8,128)(2,1)} %param.9, bf16[32,1,8,1536]{3,2,1,0:T(8,128)(2,1)} %all-to-all-done.1), kind=kLoop, calls=%fused_computation.23 | loop fusion | flops 2359296 | bytes 5505024 | tf_op jit(solution)/shard_map/convert_element_type | solution.py:70
  (25 shorter events, 1.4 us)
Async XLA Ops:
  6.5 1.4 copy-start
  6.5 67.6 %all-gather.3.cloned.1.call-start = ((), (), s32[]{:S(2)}) async-start(), calls=%async_computation.3 | async-start | bytes 3244032 | tf_op jit(solution)/shard_map/all_gather | solution.py:52
  7.3 106.2 %reduce-scatter.2.cloned.1.call-start = ((), (), s32[]{:S(2)}) async-start(), calls=%async_computation.4 | async-start | bytes 1769472 | tf_op jit(solution)/shard_map/reduce_scatter | solution.py:56
  76.8 38.3 %copy-start.1 = (bf16[1,1,256,3,1536]{4,2,3,1,0:T(8,128)(2,1)S(1)}, bf16[1,1,256,3,1536]{4,2,3,1,0:T(8,128)(2,1)}, u32[]{:S(2)}) copy-start(bf16[1,1,256,3,1536]{4,2,3,1,0:T(8,128)(2,1)} %param.7) | copy-start | bytes 7077892
  78.6 153.8 %all-gather.5.cloned.1.call-start = ((), (), s32[]{:S(2)}) async-start(), calls=%async_computation.5 | async-start | bytes 3244032 | tf_op jit(solution)/shard_map/all_gather | solution.py:58
  116.7 14.7 %copy-start.5 = (s32[8]{0:T(128)S(1)}, s32[8]{0:T(128)}, u32[]{:S(2)}) copy-start(s32[8]{0:T(128)} %param.13) | copy-start | bytes 100
  116.7 74.3 %all-to-all-start = ((bf16[1,32,8,3,1536]{4,2,3,0,1:T(8,128)(2,1)}), bf16[1,32,8,3,1536]{4,2,3,0,1:T(8,128)(2,1)}, u32[]{:S(2)}, u32[]{:S(2)}) async-start(bf16[1,32,8,3,1536]{4,2,3,0,1:T(8,128)(2,1)} %copy.55), calls=%async_computation | async-start | bytes 4718592 | tf_op jit(solution)/shard_map/all_to_all | solution.py:49
  131.4 3.9 %copy-start.6 = (s32[8]{0:T(128)S(1)}, s32[8]{0:T(128)}, u32[]{:S(2)}) copy-start(s32[8]{0:T(128)} %param.12) | copy-start | bytes 100
  131.4 4.5 %copy-start.4 = (bf16[1,1,256,1536]{3,2,1,0:T(8,128)(2,1)S(1)}, bf16[1,1,256,1536]{3,2,1,0:T(8,128)(2,1)}, u32[]{:S(2)}) copy-start(bf16[1,1,256,1536]{3,2,1,0:T(8,128)(2,1)} %param.8) | copy-start | bytes 2359300
  197.1 3.3 %copy-start.3 = (bf16[32,8,1,12,128]{4,3,1,2,0:T(8,128)(2,1)S(1)}, bf16[32,8,1,12,128]{4,3,1,2,0:T(8,128)(2,1)}, u32[]{:S(2)}) copy-start(bf16[32,8,1,12,128]{4,3,1,2,0:T(8,128)(2,1)} %get-tuple-element.27) | copy-start | bytes 2359300
  202.5 45.4 %all-to-all-start.1 = ((bf16[32,1,8,1536]{3,2,1,0:T(8,128)(2,1)}), bf16[32,1,8,1536]{3,2,1,0:T(8,128)(2,1)}, u32[]{:S(2)}, u32[]{:S(2)}) async-start(bf16[32,1,8,1536]{3,2,1,0:T(8,128)(2,1)} %bitcast.83), calls=%async_computation.1 | async-start | bytes 1572864 | tf_op jit(solution)/shard_map/all_to_all | solution.py:50
  245.9 2.0 copy-start.2
Sparse Core Ops, SparseCore 0:
  10.5 63.6 all-gather.2
  78.7 34.7 reduce-scatter.1
  116.6 115.7 all-gather.4
where the time goes:
time: 258 us; the launch traced here: 257 us
  waiting for transfers between devices  169 us (66%)
  local copies, waits for them, and re-layouts  28.5 us (11%)
  starting transfers between devices  21.5 us (8%)
  between operations  14.6 us (6%)
  matrix products  13.4 us (5%)
  other arithmetic  9.86 us (4%)
    all_gather x1, waiting for transfers between devices, body(): weight_piece = lax.all_gather(kv_weight, 'seq', axis=0, tiled=True)  64.8 us
    all_to_all x1, waiting for transfers between devices, body(): lax.all_to_all(blocked, 'seq', split_axis=1, concat_axis=0, tiled=True)  45.7 us
    reduce_scatter x1, waiting for transfers between devices, body(): lax.psum_scatter(partial_sum, 'grp', scatter_dimension=0, tiled=True)  34.9 us
    all_gather x1, waiting for transfers between devices, body(): pairs = lax.all_gather(own_rows, 'seq', axis=0, tiled=True)  23.1 us
    all_to_all x1, starting transfers between devices, body(): lax.all_to_all(blocked, 'seq', split_axis=1, concat_axis=0, tiled=True)  14.7 us
    all_gather x1, local copies, waits for them, and re-layouts, body(): pairs = lax.all_gather(own_rows, 'seq', axis=0, tiled=True)  6.99 us
    all_to_all x1, starting transfers between devices, body(): lax.all_to_all(moved, 'seq', split_axis=0, concat_axis=1, tiled=True)  6.72 us
    unnamed x17, local copies, waits for them, and re-layouts  6.33 us
  transfers between devices with their start and end apart: 5, of which 4 were waited for; matrix products, arithmetic and copies ran while one was open for 17% of the time, Pallas kernels for 0%

commit v1 on v0

v1 whole, which is shorter than its diff:
```python
import functools
import math

import jax
import jax.numpy as jnp
from jax import lax
from jax.experimental import pallas as pl
from jax.experimental.pallas import tpu as pltpu
from jax.sharding import PartitionSpec as P

HDIM = 128
SCALE = 1.0 / math.sqrt(HDIM)
MESH = pl.DeviceIdType.MESH
NX, NY, NC, NZ = 4, 4, 2, 8
ROWS = 16
FEAT = 512
CB = 768


def project_kernel(assign_ref, a_ref, w_ref, g_ref, ag, wg, part, got,
                   wx_s, wx_r, ar_s, ar_r, wr_s, wr_r, wc_s, wc_r, z_s, z_r,
                   gy_s, gy_r, gx_s, gx_r, gc_s, gc_r, loc_s):
    z = lax.axis_index("grp")
    s = lax.axis_index("seq")
    h = lax.axis_index("hd")
    x = s // 8
    y = (s // 2) % 4
    c = s % 2

    def dev(zz, xx, yy, cc):
        return (zz, (xx * 4 + yy) * 2 + cc, h)

    def put(src, dst, ss, rs, to):
        return pltpu.make_async_remote_copy(
            src_ref=src, dst_ref=dst, send_sem=ss, recv_sem=rs,
            device_id=to, device_id_type=MESH)

    barrier = pltpu.get_barrier_semaphore()
    peers = ([dev(z, (x + k) % 4, y, c) for k in (1, 2, 3)]
             + [dev(z, x, (y + k) % 4, c) for k in (1, 3)]
             + [dev(z, x, y, 1 - c)]
             + [dev((z + k) % 8, x, y, c) for k in range(1, 8)])
    for p in peers:
        pl.semaphore_signal(barrier, inc=1, device_id=p, device_id_type=MESH)
    pl.semaphore_wait(barrier, len(peers))

    def ring(me, at, lo, hi, to, ss, rs):
        left, right = (me + 3) % 4, (me + 1) % 4
        opp = (me + 2) % 4
        first = [put(at(me), at(me), ss.at[0], rs.at[0], to(right)),
                 put(at(me), at(me), ss.at[1], rs.at[1], to(left))]
        second = [put(lo(left), lo(left), ss.at[2], rs.at[2], to(right)),
                  put(hi(right), hi(right), ss.at[3], rs.at[3], to(left))]
        arrive = [put(at(left), at(left), ss.at[0], rs.at[0], to(right)),
                  put(at(right), at(right), ss.at[1], rs.at[1], to(left)),
                  put(lo(opp), lo(opp), ss.at[2], rs.at[2], to(right)),
                  put(hi(opp), hi(opp), ss.at[3], rs.at[3], to(left))]

        def start():
            first[0].start()
            first[1].start()

        def forward():
            arrive[0].wait_recv()
            second[0].start()
            arrive[1].wait_recv()
            second[1].start()

        def finish():
            arrive[2].wait_recv()
            arrive[3].wait_recv()
            for d in first + second:
                d.wait_send()

        return start, forward, finish

    own_w = pltpu.make_async_copy(w_ref.at[x], wg.at[x, y, c], loc_s.at[0])
    own_w.start()
    own_a = pltpu.make_async_copy(a_ref, ag.at[x], loc_s.at[1])
    own_a.start()
    wx = []
    for k in (1, 2, 3):
        to = (x + k) % 4
        d = put(w_ref.at[to], wg.at[x, y, c], wx_s.at[k - 1], wx_r.at[k - 1], dev(z, to, y, c))
        d.start()
        wx.append(d)
    own_a.wait()
    a_start, a_forward, a_finish = ring(
        x, lambda k: ag.at[k], lambda k: ag.at[k, 0:4], lambda k: ag.at[k, 4:8],
        lambda k: dev(z, k, y, c), ar_s, ar_r)
    a_start()
    own_w.wait()
    for k in (1, 2, 3):
        frm = (x + 4 - k) % 4
        put(w_ref.at[x], wg.at[frm, y, c], wx_s.at[k - 1], wx_r.at[k - 1],
            dev(z, frm, y, c)).wait_recv()
    w_start, w_forward, w_finish = ring(
        y, lambda k: wg.at[:, k, c], lambda k: wg.at[0:2, k, c], lambda k: wg.at[2:4, k, c],
        lambda k: dev(z, x, k, c), wr_s, wr_r)
    w_start()
    a_forward()
    w_forward()
    a_finish()
    w_finish()
    swap = put(wg.at[:, :, c], wg.at[:, :, c], wc_s, wc_r, dev(z, x, y, 1 - c))
    swap.start()
    put(wg.at[:, :, 1 - c], wg.at[:, :, 1 - c], wc_s, wc_r, dev(z, x, y, 1 - c)).wait_recv()

    for half in range(2):
        lhs = jnp.concatenate(
            [ag[xb, assign_ref[half * 4 + j]] for j in range(4) for xb in range(4)], axis=0)
        rhs = wg[...].reshape(FEAT, CB)
        prod = jnp.dot(lhs, rhs, preferred_element_type=jnp.float32)
        part[half * 4:half * 4 + 4] = prod.astype(jnp.bfloat16).reshape(4, 64, CB)
    sent = []
    for k in (4, 3, 5, 2, 6, 1, 7):
        to = (z + k) % 8
        d = put(part.at[to], got.at[k - 1], z_s.at[k - 1], z_r.at[k - 1], dev(to, x, y, c))
        d.start()
        sent.append(d)
    for d in wx:
        d.wait_send()
    swap.wait_send()
    total = part[z].astype(jnp.float32)
    for k in range(1, 8):
        frm = (z + 8 - k) % 8
        put(part.at[0], got.at[k - 1], z_s.at[k - 1], z_r.at[k - 1], dev(frm, x, y, c)).wait_recv()
        total = total + got[k - 1].astype(jnp.float32)
    g_ref[x, y, c] = total.astype(jnp.bfloat16)

    y_start, y_forward, y_finish = ring(
        y, lambda k: g_ref.at[x, k, c], lambda k: g_ref.at[x, k, c, 0:32],
        lambda k: g_ref.at[x, k, c, 32:64], lambda k: dev(z, x, k, c), gy_s, gy_r)
    y_start()
    y_forward()
    y_finish()
    x_start, x_forward, x_finish = ring(
        x, lambda k: g_ref.at[k, :, c], lambda k: g_ref.at[k, 0:2, c],
        lambda k: g_ref.at[k, 2:4, c], lambda k: dev(z, k, y, c), gx_s, gx_r)

    def to_core(k, i):
        return put(g_ref.at[k, :, c], g_ref.at[k, :, c], gc_s.at[i], gc_r.at[i], dev(z, x, y, 1 - c))

    x_start()
    swaps = [to_core((x + k) % 4, i) for i, k in enumerate((0, 3, 1, 2))]
    swaps[0].start()
    x_forward()
    swaps[1].start()
    swaps[2].start()
    x_finish()
    swaps[3].start()
    for d in sent:
        d.wait_send()
    for i, k in enumerate((0, 3, 1, 2)):
        b = (x + k) % 4
        put(g_ref.at[b, :, 1 - c], g_ref.at[b, :, 1 - c], gc_s.at[i], gc_r.at[i],
            dev(z, x, y, 1 - c)).wait_recv()
    for d in swaps:
        d.wait_send()


def project(assignment, prompts, weight):
    sem = pltpu.SemaphoreType.DMA
    vm = pl.BlockSpec(memory_space=pltpu.VMEM)
    return pl.pallas_call(
        project_kernel,
        out_shape=jax.ShapeDtypeStruct((NX, NY, NC, 64, CB), jnp.bfloat16),
        in_specs=[pl.BlockSpec(memory_space=pltpu.SMEM), vm, vm],
        out_specs=vm,
        scratch_shapes=[
            pltpu.VMEM((NX, 8, ROWS, FEAT), jnp.bfloat16),
            pltpu.VMEM((NX, NY, NC, ROWS, CB), jnp.bfloat16),
            pltpu.VMEM((NZ, 64, CB), jnp.bfloat16),
            pltpu.VMEM((NZ - 1, 64, CB), jnp.bfloat16),
            sem((3,)), sem((3,)), sem((4,)), sem((4,)), sem((4,)), sem((4,)),
            sem, sem, sem((7,)), sem((7,)),
            sem((4,)), sem((4,)), sem((4,)), sem((4,)), sem((4,)), sem((4,)), sem((2,)),
        ],
        compiler_params=pltpu.CompilerParams(
            collective_id=0, has_side_effects=True, vmem_limit_bytes=24 * 2**20),
        cost_estimate=pl.CostEstimate(flops=2 * 10**8, bytes_accessed=8 * 10**6, transcendentals=0),
        name="project",
    )(assignment, prompts, weight)


def soft(scores):
    top = jnp.max(scores, axis=-1, keepdims=True)
    powered = jnp.exp(scores - top)
    return (powered * (1.0 / jnp.sum(powered, axis=-1, keepdims=True))).astype(jnp.bfloat16)


def qk(q, k):
    return lax.dot_general(q, k, (((1,), (1,)), ((), ())), preferred_element_type=jnp.float32) * SCALE


def spatial_kernel(lat_ref, res_ref, out_ref):
    for i in range(2):
        cols = slice(i * HDIM, (i + 1) * HDIM)
        w = soft(qk(lat_ref[0, :, cols], lat_ref[1, :, cols]))
        o = jnp.dot(w, lat_ref[2, :, cols], preferred_element_type=jnp.float32)
        out_ref[:, cols] = res_ref[:, cols].astype(jnp.float32) + o


def spatial_part(latent, residual):
    wide = 2 * HDIM
    return pl.pallas_call(
        spatial_kernel,
        out_shape=jax.ShapeDtypeStruct(residual.shape, jnp.float32),
        grid=(residual.shape[1] // wide,),
        in_specs=[pl.BlockSpec((3, 256, wide), lambda i: (0, 0, i)),
                  pl.BlockSpec((256, wide), lambda i: (0, i))],
        out_specs=pl.BlockSpec((256, wide), lambda i: (0, i)),
        cost_estimate=pl.CostEstimate(flops=10**7, bytes_accessed=5 * 10**6, transcendentals=10**6),
        name="spatial",
    )(latent, residual)


def temporal_kernel(in_ref, out_ref):
    row = lax.broadcasted_iota(jnp.int32, (256, 256), 0) % 8
    col = lax.broadcasted_iota(jnp.int32, (256, 256), 1) % 8
    for i in range(2):
        cols = slice(i * HDIM, (i + 1) * HDIM)
        q, k, v = (in_ref[:, j, :, cols].reshape(256, HDIM) for j in range(3))
        w = soft(jnp.where(row == col, qk(q, k), -1e30))
        o = jnp.dot(w, v, preferred_element_type=jnp.float32)
        out_ref[:, :, cols] = o.astype(jnp.bfloat16).reshape(32, 8, HDIM)


def temporal_part(moved):
    wide = 2 * HDIM
    return pl.pallas_call(
        temporal_kernel,
        out_shape=jax.ShapeDtypeStruct((32, 8, moved.shape[3]), jnp.bfloat16),
        grid=(moved.shape[3] // wide,),
        in_specs=[pl.BlockSpec((32, 3, 8, wide), lambda i: (0, 0, 0, i))],
        out_specs=pl.BlockSpec((32, 8, wide), lambda i: (0, 0, i)),
        cost_estimate=pl.CostEstimate(flops=10**7, bytes_accessed=5 * 10**6, transcendentals=10**6),
        name="temporal",
    )(moved)


def cross_kernel(len_ref, q_ref, k_ref, v_ref, acc_ref, out_ref):
    r = lax.broadcasted_iota(jnp.int32, (1, 512), 1)
    yy, cc, xb, i = r // 128, (r // 64) % 2, (r // 16) % 4, r % 16
    pos = ((xb * 4 + yy) * 2 + cc) * 16 + i
    bias = jnp.where(pos < len_ref[0], 0.0, -1e9)
    for i in range(2):
        cols = slice(i * HDIM, (i + 1) * HDIM)
        w = soft(qk(q_ref[:, cols], k_ref[0, :, cols]) + bias)
        o = jnp.dot(w, v_ref[0, :, cols], preferred_element_type=jnp.float32)
        out_ref[:, cols] = acc_ref[:, cols] + o


def cross_part(length, query, pairs, acc):
    wide = 2 * HDIM
    return pl.pallas_call(
        cross_kernel,
        out_shape=jax.ShapeDtypeStruct(acc.shape, jnp.float32),
        grid=(acc.shape[1] // wide,),
        in_specs=[pl.BlockSpec(memory_space=pltpu.SMEM),
                  pl.BlockSpec((256, wide), lambda i: (0, i)),
                  pl.BlockSpec((1, 512, wide), lambda i: (i // 3, 0, i % 3)),
                  pl.BlockSpec((1, 512, wide), lambda i: (2 + i // 3, 0, i % 3)),
                  pl.BlockSpec((256, wide), lambda i: (0, i))],
        out_specs=pl.BlockSpec((256, wide), lambda i: (0, i)),
        cost_estimate=pl.CostEstimate(flops=10**7, bytes_accessed=8 * 10**6, transcendentals=10**6),
        name="cross",
    )(length, query, pairs, pairs, acc)


def body(latent_qkv, cross_query, residual, prompt_states, kv_weight, prompt_lengths, assignment):
    latent = jnp.transpose(latent_qkv[0, 0], (1, 0, 2))
    blocked = jnp.transpose(latent.reshape(3, 32, 8, 1536), (1, 0, 2, 3))
    moved = lax.all_to_all(blocked, "seq", split_axis=0, concat_axis=0, tiled=True)
    weight = jnp.transpose(kv_weight.reshape(ROWS, 4, CB), (1, 0, 2))
    pairs = project(assignment, prompt_states, weight)
    acc = spatial_part(latent, residual[0, 0])
    moved, pairs, acc = lax.optimization_barrier((moved, pairs, acc))
    returned = lax.all_to_all(temporal_part(moved), "seq", split_axis=0, concat_axis=0, tiled=True)
    served = assignment[lax.axis_index("grp")]
    length = lax.dynamic_slice(prompt_lengths, (served,), (1,))
    acc = cross_part(length, cross_query[0, 0], pairs.reshape(4, 512, CB), acc)
    total = acc + returned.reshape(256, 1536).astype(jnp.float32)
    return total.astype(jnp.bfloat16)[None, None]


def solution(mesh):
    return jax.shard_map(
        body,
        mesh=mesh,
        in_specs=(
            P("grp", "seq", None, None, "hd"),
            P("grp", "seq", None, "hd"),
            P("grp", "seq", None, "hd"),
            P(None, "seq", "grp"),
            P(("grp", "seq"), None, "hd"),
            P(),
            P(),
        ),
        out_specs=P("grp", "seq", None, "hd"),
        check_vma=False,
    )
```

time: 258 us -> 181 us (0.70)
  the two profiles are of different devices: /device:TPU:321 before, /device:TPU:1 now
where the time goes in v1:
time: 181 us
  Pallas kernels  136 us (75%)
  starting transfers between devices  21.2 us (12%)
  waiting for transfers between devices  11.3 us (6%)
  local copies, waits for them, and re-layouts  7.68 us (4%)
  other arithmetic  2.47 us (1%)
  between operations  1.98 us (1%)
    pallas_call x1, Pallas kernels, project(): pl.pallas_call(project_kernel, out_shape=jax.ShapeDtypeStruct((NX, NY, NC...  111 us
    all_to_all x1, waiting for transfers between devices, body(): lax.all_to_all(temporal_part(moved), 'seq', split_axis=0, concat_axis=0,...  11.3 us
    all_to_all x1, starting transfers between devices, body(): lax.all_to_all(blocked, 'seq', split_axis=0, concat_axis=0, tiled=True)  11.3 us
    all_to_all x1, starting transfers between devices, body(): lax.all_to_all(temporal_part(moved), 'seq', split_axis=0, concat_axis=0,...  9.87 us
    pallas_call x1, Pallas kernels, cross_part(): pl.pallas_call(cross_kernel, out_shape=jax.ShapeDtypeStruct(acc.shape, jn...  9.16 us
    pallas_call x1, Pallas kernels, spatial_part(): pl.pallas_call(spatial_kernel, out_shape=jax.ShapeDtypeStruct(residual.sh...  7.85 us
    pallas_call x1, Pallas kernels, temporal_part(): pl.pallas_call(temporal_kernel, out_shape=jax.ShapeDtypeStruct((32, 8, mo...  7.47 us
  transfers between devices with their start and end apart: 2, of which 1 were waited for; matrix products, arithmetic and copies ran while one was open for 1% of the time, Pallas kernels for 71%

profile of v1, /device:TPU:1, one launch (start us, length us, event | category | flops | bytes accessed | tf_op | source)
XLA Modules:
  0.0 180.5 jit_solution(1547699836335361080)
XLA Ops:
  0.0 3.3 %copy_bitcast_fusion = bf16[32,3,8,1536]{3,2,1,0:T(8,128)(2,1)} fusion(bf16[1,1,256,3,1536]{4,2,3,1,0:T(8,128)(2,1)} %param.7), kind=kLoop, calls=%fused_computation | loop fusion | bytes 4718592 | tf_op jit(solution)/shard_map/transpose | solution.py:273
  3.3 0.0 copy-start.4
  3.3 11.3 %all-to-all-start = ((bf16[32,3,8,1536]{3,2,1,0:T(8,128)(2,1)}), bf16[32,3,8,1536]{3,2,1,0:T(8,128)(2,1)S(1)}, u32[]{:S(2)}, u32[]{:S(2)}) async-start(bf16[32,3,8,1536]{3,2,1,0:T(8,128)(2,1)} %copy_bitcast_fusion), calls=%async_computation | async-start | bytes 4718592 | tf_op jit(solution)/shard_map/all_to_all | solution.py:274
  14.7 0.0 copy-done.4
  14.7 0.0 copy-start.1
  14.7 0.0 copy-start.2
  14.7 7.8 %spatial.1.acc_ref = f32[256,1536]{1,0:T(8,128)} custom-call(bf16[3,256,1536]{2,1,0:T(8,128)(2,1)} %bitcast.24, bf16[256,1536]{1,0:T(8,128)(2,1)} %bitcast.25), custom_call_target="tpu_custom_call" | custom-call | flops 10000000 | bytes 5000000 | tf_op jit(solution)/shard_map/spatial/pallas_call | solution.py:206
  22.6 0.0 copy-done.1
  22.6 0.0 copy-done.2
  22.6 111.4 %project.1 = bf16[4,4,2,64,768]{4,3,2,1,0:T(8,128)(2,1)S(1)} custom-call(s32[8]{0:T(128)S(1)} %copy-done.2, bf16[8,16,512]{2,1,0:T(8,128)(2,1)S(1)} %copy-done.1, bf16[4,16,768]{2,1,0:T(8,128)(2,1)S(1)} %bitcast.23), custom_call_target="tpu_custom_call" | custom-call | flops 200000000 | bytes 8000000 | tf_op jit(solution)/shard_map/project/pallas_call | solution.py:165
  134.0 0.0 copy-start
  134.0 1.6 copy-done
  135.6 0.0 copy-start.5
  135.6 0.0 all-to-all-done.in_ref
  135.6 0.0 copy-start.3
  135.6 1.5 copy-done.3
  137.1 7.5 %temporal.1 = bf16[32,8,1536]{2,1,0:T(8,128)(2,1)} custom-call(bf16[32,3,8,1536]{3,2,1,0:T(8,128)(2,1)} %copy-done.3), custom_call_target="tpu_custom_call" | custom-call | flops 10000000 | bytes 5000000 | tf_op jit(solution)/shard_map/temporal/pallas_call | solution.py:231
  144.6 9.9 %all-to-all-start.1 = ((bf16[32,8,1536]{2,1,0:T(8,128)(2,1)}), bf16[32,8,1536]{2,1,0:T(8,128)(2,1)S(1)}, u32[]{:S(2)}, u32[]{:S(2)}) async-start(bf16[32,8,1536]{2,1,0:T(8,128)(2,1)} %temporal.1), calls=%async_computation.1 | async-start | bytes 1572864 | tf_op jit(solution)/shard_map/all_to_all | solution.py:279
  154.4 0.6 dynamic_slice.6
  157.0 0.0 copy-done.5
  157.0 0.6 dynamic_slice.7.len_ref
  157.5 9.2 %cross.1 = f32[256,1536]{1,0:T(8,128)} custom-call(s32[1]{0:T(128)} %dynamic_slice.7.len_ref, bf16[256,1536]{1,0:T(8,128)(2,1)} %bitcast.26, bf16[4,512,768]{2,1,0:T(8,128)(2,1)} %bitcast.21, bf16[4,512,768]{2,1,0:T(8,128)(2,1)} %bitcast.22, f32[256,1536]{1,0:T(8,128)} %spatial.1.acc_ref), custom_call_target="tpu_custom_call" | custom-call | flops 10000000 | bytes 8000000 | tf_op jit(solution)/shard_map/cross/pallas_call | solution.py:256
  166.7 11.3 %all-to-all-done.1 = bf16[32,8,1536]{2,1,0:T(8,128)(2,1)S(1)} async-done(((bf16[32,8,1536]{2,1,0:T(8,128)(2,1)}), bf16[32,8,1536]{2,1,0:T(8,128)(2,1)S(1)}, u32[]{:S(2)}, u32[]{:S(2)}) %all-to-all-start.1) | async-done | bytes 786464 | tf_op jit(solution)/shard_map/all_to_all | solution.py:279
  178.1 2.5 %fusion.1 = bf16[1,1,256,1536]{3,2,1,0:T(8,128)(2,1)} fusion(f32[256,1536]{1,0:T(8,128)} %cross.1, bf16[32,8,1536]{2,1,0:T(8,128)(2,1)S(1)} %all-to-all-done.1), kind=kLoop, calls=%fused_computation.3 | loop fusion | flops 1179648 | bytes 3145728 | tf_op jit(solution)/shard_map/broadcast_in_dim | solution.py:284
  (2 shorter events, 0.0 us)
Async XLA Ops:
  3.3 11.3 %copy-start.4 = (bf16[16,2,1536]{2,1,0:T(2,128)(2,1)S(1)}, bf16[16,2,1536]{2,1,0:T(2,128)(2,1)}, u32[]{:S(2)}) copy-start(bf16[16,2,1536]{2,1,0:T(2,128)(2,1)} %param.11) | copy-start | bytes 294916
  3.3 132.3 %all-to-all-start = ((bf16[32,3,8,1536]{3,2,1,0:T(8,128)(2,1)}), bf16[32,3,8,1536]{3,2,1,0:T(8,128)(2,1)S(1)}, u32[]{:S(2)}, u32[]{:S(2)}) async-start(bf16[32,3,8,1536]{3,2,1,0:T(8,128)(2,1)} %copy_bitcast_fusion), calls=%async_computation | async-start | bytes 4718592 | tf_op jit(solution)/shard_map/all_to_all | solution.py:274
  14.7 7.9 %copy-start.1 = (bf16[8,16,512]{2,1,0:T(8,128)(2,1)S(1)}, bf16[8,16,512]{2,1,0:T(8,128)(2,1)}, u32[]{:S(2)}) copy-start(bf16[8,16,512]{2,1,0:T(8,128)(2,1)} %a_ref.1) | copy-start | bytes 393220
  14.7 7.9 %copy-start.2 = (s32[8]{0:T(128)S(1)}, s32[8]{0:T(128)}, u32[]{:S(2)}) copy-start(s32[8]{0:T(128)} %assign_ref.1) | copy-start | bytes 100
  134.0 1.6 copy-start
  135.6 21.4 %copy-start.5 = (s32[8]{0:T(128)S(1)}, s32[8]{0:T(128)}, u32[]{:S(2)}) copy-start(s32[8]{0:T(128)} %param.12) | copy-start | bytes 100
  135.6 1.5 copy-start.3
  144.6 33.5 %all-to-all-start.1 = ((bf16[32,8,1536]{2,1,0:T(8,128)(2,1)}), bf16[32,8,1536]{2,1,0:T(8,128)(2,1)S(1)}, u32[]{:S(2)}, u32[]{:S(2)}) async-start(bf16[32,8,1536]{2,1,0:T(8,128)(2,1)} %temporal.1), calls=%async_computation.1 | async-start | bytes 1572864 | tf_op jit(solution)/shard_map/all_to_all | solution.py:279

commit v2 on v0

v2 whole, which is shorter than its diff:
```python
import math

import jax
import jax.numpy as jnp
from jax import lax
from jax.experimental import pallas as pl
from jax.experimental.pallas import tpu as pltpu
from jax.sharding import PartitionSpec as P

HDIM = 128
SCALE = 1.0 / math.sqrt(HDIM)
MESH = pl.DeviceIdType.MESH
ROWS, FEAT, CB, HALF = 16, 512, 768, 768


def soft(scores):
    top = jnp.max(scores, axis=-1, keepdims=True)
    powered = jnp.exp(scores - top)
    return (powered * (1.0 / jnp.sum(powered, axis=-1, keepdims=True))).astype(jnp.bfloat16)


def qk(q, k):
    return lax.dot_general(q, k, (((1,), (1,)), ((), ())), preferred_element_type=jnp.float32) * SCALE


def lanes(i):
    return pl.ds(pl.multiple_of(i * HDIM, HDIM), HDIM)


def block_kernel(assign_ref, len_ref, lat_ref, cq_ref, res_ref, a_ref, w_ref, out_ref,
                 lat, cq, res, acc, mv0, mv1, t0, t1, rt0, rt1, ag, wg, part, got, g,
                 loc, ex_s, ex_r, rt_s, rt_r,
                 wx_s, wx_r, ar_s, ar_r, wr_s, wr_r, wc_s, wc_r, z_s, z_r,
                 gy_s, gy_r, gx_s, gx_r, gc_s, gc_r):
    z = lax.axis_index("grp")
    s = lax.axis_index("seq")
    h = lax.axis_index("hd")
    x = s // 8
    y = (s // 2) % 4
    c = s % 2

    def dev(zz, xx, yy, cc):
        return (zz, (xx * 4 + yy) * 2 + cc, h)

    def put(src, dst, ss, rs, to):
        return pltpu.make_async_remote_copy(
            src_ref=src, dst_ref=dst, send_sem=ss, recv_sem=rs,
            device_id=to, device_id_type=MESH)

    def peer(t):
        return (((x + t // 8) % 4) * 4 + (y + t) % 4) * 2 + (c + t // 4) % 2

    mvs, ts, rts = (mv0, mv1), (t0, t1), (rt0, rt1)
    cols = (pl.ds(0, HALF), pl.ds(HALF, HALF))
    local = [
        pltpu.make_async_copy(w_ref.at[x], wg.at[x, y, c], loc.at[0]),
        pltpu.make_async_copy(a_ref, ag.at[x], loc.at[1]),
        pltpu.make_async_copy(lat_ref, lat, loc.at[2]),
        pltpu.make_async_copy(res_ref, res, loc.at[3]),
        pltpu.make_async_copy(lat_ref.at[:, s, :, cols[0]], mv0.at[s], loc.at[4]),
        pltpu.make_async_copy(lat_ref.at[:, s, :, cols[1]], mv1.at[s], loc.at[5]),
        pltpu.make_async_copy(cq_ref, cq, loc.at[6]),
    ]
    for d in local:
        d.start()

    barrier = pltpu.get_barrier_semaphore()

    @pl.loop(1, 32)
    def _(t):
        pl.semaphore_signal(barrier, inc=1, device_id=(z, peer(t), h), device_id_type=MESH)

    @pl.loop(1, 8)
    def _(k):
        pl.semaphore_signal(barrier, inc=1, device_id=((z + k) % 8, s, h), device_id_type=MESH)

    pl.semaphore_wait(barrier, 38)

    def ring(me, at, lo, hi, to, ss, rs):
        left, right = (me + 3) % 4, (me + 1) % 4
        opp = (me + 2) % 4
        first = [put(at(me), at(me), ss.at[0], rs.at[0], to(right)),
                 put(at(me), at(me), ss.at[1], rs.at[1], to(left))]
        second = [put(lo(left), lo(left), ss.at[2], rs.at[2], to(right)),
                  put(hi(right), hi(right), ss.at[3], rs.at[3], to(left))]
        arrive = [put(at(left), at(left), ss.at[0], rs.at[0], to(right)),
                  put(at(right), at(right), ss.at[1], rs.at[1], to(left)),
                  put(lo(opp), lo(opp), ss.at[2], rs.at[2], to(right)),
                  put(hi(opp), hi(opp), ss.at[3], rs.at[3], to(left))]

        def start():
            first[0].start()
            first[1].start()

        def forward():
            arrive[0].wait_recv()
            second[0].start()
            arrive[1].wait_recv()
            second[1].start()

        def finish():
            arrive[2].wait_recv()
            arrive[3].wait_recv()

        def drain():
            for d in first + second:
                d.wait_send()

        return start, forward, finish, drain

    def exchange(half, lo, hi):
        @pl.loop(lo, hi)
        def _(t):
            to = peer(t)
            put(lat_ref.at[:, to, :, cols[half]], mvs[half].at[s],
                ex_s.at[half], ex_r.at[half], (z, to, h)).start()

    def give_back(half):
        @pl.loop(1, 32)
        def _(t):
            to = peer(t)
            put(ts[half].at[to], rts[half].at[s], rt_s.at[half], rt_r.at[half], (z, to, h)).start()

    def all_of(ref, ss, rs, half):
        whole = ref.at[pl.ds(0, 31)]
        return put(whole, whole, ss.at[half], rs.at[half], (z, peer(1), h))

    def spatial(lo, hi):
        @pl.loop(lo, hi)
        def _(i):
            for j in range(2):
                at = lanes(i * 2 + j)
                q, k, v = (lat[n, :, :, at].reshape(256, HDIM) for n in range(3))
                o = jnp.dot(soft(qk(q, k)), v, preferred_element_type=jnp.float32)
                acc[:, at] = res[:, at].astype(jnp.float32) + o

    def temporal(half):
        mv, t = mvs[half], ts[half]
        row = lax.broadcasted_iota(jnp.int32, (256, 256), 0) % 8
        col = lax.broadcasted_iota(jnp.int32, (256, 256), 1) % 8

        @pl.loop(0, 3)
        def _(i):
            for j in range(2):
                at = lanes(i * 2 + j)
                q, k, v = (mv[:, n, :, at].reshape(256, HDIM) for n in range(3))
                w = soft(jnp.where(row == col, qk(q, k), -1e30))
                o = jnp.dot(w, v, preferred_element_type=jnp.float32)
                t[:, :, at] = o.astype(jnp.bfloat16).reshape(32, 8, HDIM)

        rts[half][pl.ds(s, 1)] = t[pl.ds(s, 1)]

    r = lax.broadcasted_iota(jnp.int32, (1, 512), 1)
    pos = ((((r // 16) % 4) * 4 + r // 128) * 2 + (r // 64) % 2) * 16 + r % 16
    bias = jnp.where(pos < len_ref[assign_ref[z]], 0.0, -1e9)

    def cross(b):
        for j in range(3):
            at = lanes(b * 3 + j)
            k = g[b, :, :, :, j * HDIM:(j + 1) * HDIM].reshape(512, HDIM)
            v = g[b, :, :, :, 384 + j * HDIM:384 + (j + 1) * HDIM].reshape(512, HDIM)
            w = soft(qk(cq[:, at], k) + bias)
            acc[:, at] = acc[:, at] + jnp.dot(w, v, preferred_element_type=jnp.float32)

    wx = []
    for k in (1, 2, 3):
        to = (x + k) % 4
        d = put(w_ref.at[to], wg.at[x, y, c], wx_s.at[k - 1], wx_r.at[k - 1], dev(z, to, y, c))
        d.start()
        wx.append(d)
    local[1].wait()
    a_start, a_forward, a_finish, a_drain = ring(
        x, lambda k: ag.at[k], lambda k: ag.at[k, 0:4], lambda k: ag.at[k, 4:8],
        lambda k: dev(z, k, y, c), ar_s, ar_r)
    a_start()
    exchange(0, 1, 8)
    local[0].wait()
    for k in (1, 2, 3):
        frm = (x + 4 - k) % 4
        put(w_ref.at[x], wg.at[frm, y, c], wx_s.at[k - 1], wx_r.at[k - 1],
            dev(z, frm, y, c)).wait_recv()
    w_start, w_forward, w_finish, w_drain = ring(
        y, lambda k: wg.at[:, k, c], lambda k: wg.at[0:2, k, c], lambda k: wg.at[2:4, k, c],
        lambda k: dev(z, x, k, c), wr_s, wr_r)
    w_start()
    exchange(0, 8, 16)
    local[2].wait()
    local[3].wait()
    spatial(0, 2)
    a_forward()
    w_forward()
    exchange(0, 16, 32)
    exchange(1, 1, 8)
    spatial(2, 6)
    a_finish()
    w_finish()
    swap = put(wg.at[:, :, c], wg.at[:, :, c], wc_s, wc_r, dev(z, x, y, 1 - c))
    swap.start()
    put(wg.at[:, :, 1 - c], wg.at[:, :, 1 - c], wc_s, wc_r, dev(z, x, y, 1 - c)).wait_recv()

    for half in range(2):
        lhs = jnp.concatenate(
            [ag[xb, assign_ref[half * 4 + j]] for j in range(4) for xb in range(4)], axis=0)
        prod = jnp.dot(lhs, wg[...].reshape(FEAT, CB), preferred_element_type=jnp.float32)
        part[half * 4:half * 4 + 4] = prod.astype(jnp.bfloat16).reshape(4, 64, CB)
    sent = []
    for k in (4, 3, 5, 2, 6, 1, 7):
        to = (z + k) % 8
        d = put(part.at[to], got.at[k - 1], z_s.at[k - 1], z_r.at[k - 1], dev(to, x, y, c))
        d.start()
        sent.append(d)

    exchange(1, 8, 20)
    all_of(mv0, ex_s, ex_r, 0).wait_recv()
    local[4].wait()
    temporal(0)

    total = part[z].astype(jnp.float32)
    for k in range(1, 8):
        frm = (z + 8 - k) % 8
        put(part.at[0], got.at[k - 1], z_s.at[k - 1], z_r.at[k - 1], dev(frm, x, y, c)).wait_recv()
        total = total + got[k - 1].astype(jnp.float32)
    g[x, y, c] = total.astype(jnp.bfloat16)

    y_start, y_forward, y_finish, y_drain = ring(
        y, lambda k: g.at[x, k, c], lambda k: g.at[x, k, c, 0:32],
        lambda k: g.at[x, k, c, 32:64], lambda k: dev(z, x, k, c), gy_s, gy_r)
    x_start, x_forward, x_finish, x_drain = ring(
        x, lambda k: g.at[k, :, c], lambda k: g.at[k, 0:2, c],
        lambda k: g.at[k, 2:4, c], lambda k: dev(z, k, y, c), gx_s, gx_r)
    blocks = [(x + k) % 4 for k in (0, 3, 1, 2)]
    swaps = [put(g.at[b, :, c], g.at[b, :, c], gc_s.at[i], gc_r.at[i], dev(z, x, y, 1 - c))
             for i, b in enumerate(blocks)]
    swapped = [put(g.at[b, :, 1 - c], g.at[b, :, 1 - c], gc_s.at[i], gc_r.at[i],
                   dev(z, x, y, 1 - c)) for i, b in enumerate(blocks)]
    y_start()
    exchange(1, 20, 32)
    y_forward()
    give_back(0)
    y_finish()
    x_start()
    swaps[0].start()
    local[6].wait()
    swapped[0].wait_recv()
    cross(blocks[0])

    all_of(mv1, ex_s, ex_r, 1).wait_recv()
    local[5].wait()
    temporal(1)
    give_back(1)

    x_forward()
    swaps[1].start()
    swaps[2].start()
    swapped[1].wait_recv()
    cross(blocks[1])
    swapped[2].wait_recv()
    cross(blocks[2])
    x_finish()
    swaps[3].start()
    swapped[3].wait_recv()
    cross(blocks[3])

    for half in range(2):
        all_of(rts[half], rt_s, rt_r, half).wait_recv()
        back = rts[half][...].reshape(256, HALF).astype(jnp.float32)
        out_ref[:, cols[half]] = (acc[:, cols[half]] + back).astype(jnp.bfloat16)

    for half in range(2):
        all_of(mvs[half], ex_s, ex_r, half).wait_send()
        all_of(ts[half], rt_s, rt_r, half).wait_send()
    for d in wx + [swap] + sent + swaps:
        d.wait_send()
    a_drain()
    w_drain()
    y_drain()
    x_drain()


def body(latent_qkv, cross_query, residual, prompt_states, kv_weight, prompt_lengths, assignment):
    latent = jnp.transpose(latent_qkv[0, 0], (1, 0, 2)).reshape(3, 32, 8, 1536)
    weight = jnp.transpose(kv_weight.reshape(ROWS, 2, 4, 384), (2, 0, 1, 3)).reshape(4, ROWS, CB)
    sem = pltpu.SemaphoreType.DMA
    vm = pl.BlockSpec(memory_space=pltpu.VMEM)
    sm = pl.BlockSpec(memory_space=pltpu.SMEM)
    hb = pl.BlockSpec(memory_space=pl.ANY)
    b16, f32 = jnp.bfloat16, jnp.float32
    out = pl.pallas_call(
        block_kernel,
        out_shape=jax.ShapeDtypeStruct((256, 1536), b16),
        in_specs=[sm, sm, hb, hb, hb, vm, vm],
        out_specs=vm,
        scratch_shapes=[
            pltpu.VMEM((3, 32, 8, 1536), b16),
            pltpu.VMEM((256, 1536), b16),
            pltpu.VMEM((256, 1536), b16),
            pltpu.VMEM((256, 1536), f32),
            pltpu.VMEM((32, 3, 8, HALF), b16), pltpu.VMEM((32, 3, 8, HALF), b16),
            pltpu.VMEM((32, 8, HALF), b16), pltpu.VMEM((32, 8, HALF), b16),
            pltpu.VMEM((32, 8, HALF), b16), pltpu.VMEM((32, 8, HALF), b16),
            pltpu.VMEM((4, 8, ROWS, FEAT), b16),
            pltpu.VMEM((4, 4, 2, ROWS, CB), b16),
            pltpu.VMEM((8, 64, CB), b16),
            pltpu.VMEM((7, 64, CB), b16),
            pltpu.VMEM((4, 4, 2, 64, CB), b16),
            sem((7,)), sem((2,)), sem((2,)), sem((2,)), sem((2,)),
            sem((3,)), sem((3,)), sem((4,)), sem((4,)), sem((4,)), sem((4,)),
            sem, sem, sem((7,)), sem((7,)),
            sem((4,)), sem((4,)), sem((4,)), sem((4,)), sem((4,)), sem((4,)),
        ],
        compiler_params=pltpu.CompilerParams(collective_id=0, has_side_effects=True),
        name="block",
    )(assignment, prompt_lengths, latent, cross_query[0, 0], residual[0, 0], prompt_states, weight)
    return out[None, None]


def solution(mesh):
    return jax.shard_map(
        body,
        mesh=mesh,
        in_specs=(
            P("grp", "seq", None, None, "hd"),
            P("grp", "seq", None, "hd"),
            P("grp", "seq", None, "hd"),
            P(None, "seq", "grp"),
            P(("grp", "seq"), None, "hd"),
            P(),
            P(),
        ),
        out_specs=P("grp", "seq", None, "hd"),
        check_vma=False,
    )
```

time: 258 us -> 119 us (0.46)
  the two profiles are of different devices: /device:TPU:321 before, /device:TPU:1 now
where the time goes in v2:
time: 119 us; the launch traced here: 118 us
  Pallas kernels  115 us (97%)
  local copies, waits for them, and re-layouts  3.73 us (3%)
    pallas_call x1, Pallas kernels, body(): pl.pallas_call(block_kernel, out_shape=jax.ShapeDtypeStruct((256, 1536),...  115 us

profile of v2, /device:TPU:1, one launch (start us, length us, event | category | flops | bytes accessed | tf_op | source)
XLA Modules:
  0.0 118.3 jit_solution(6850070219296261576)
XLA Ops:
  0.0 1.0 copy.11
  1.0 0.7 reshape.11.w_ref
  1.7 114.6 %block.1 = bf16[256,1536]{1,0:T(8,128)(2,1)} custom-call(s32[8]{0:T(128)} %assign_ref.1, s32[8]{0:T(128)} %len_ref.1, bf16[3,32,8,1536]{3,2,1,0:T(8,128)(2,1)} %bitcast.16, bf16[256,1536]{1,0:T(8,128)(2,1)} %bitcast.17, bf16[256,1536]{1,0:T(8,128)(2,1)} %bitcast.18, bf16[8,16,512]{2,1,0:T(8,128)(2,1)} %a_ref.1, bf16[4,16,768]{2,1,0:T(8,128)(2,1)} %reshape.11.w_ref), custom_call_target="tpu_custom_call" | custom-call | tf_op jit(solution)/shard_map/block/pallas_call | solution.py:288
  116.3 2.1 %copy.13 = bf16[1,1,256,1536]{3,2,1,0:T(8,128)(2,1)} copy(bf16[1,1,256,1536]{3,2,1,0:T(8,128)(2,1)} %bitcast.15) | data formatting | bytes 1572864

commit v3 on v2

--- a/solution.py
+++ b/solution.py
@@ -27,8 +27,8 @@
     return pl.ds(pl.multiple_of(i * HDIM, HDIM), HDIM)
 
 
-def block_kernel(assign_ref, len_ref, lat_ref, cq_ref, res_ref, a_ref, w_ref, out_ref,
-                 lat, cq, res, acc, mv0, mv1, t0, t1, rt0, rt1, ag, wg, part, got, g,
+def block_kernel(assign_ref, len_ref, lat_ref, cq_ref, res_ref, a_ref, raw_ref, out_ref,
+                 w_ref, lat, cq, res, acc, mv0, mv1, t0, t1, rt0, rt1, ag, wg, part0, part1, got0, got1, g0, g1,
                  loc, ex_s, ex_r, rt_s, rt_r,
                  wx_s, wx_r, ar_s, ar_r, wr_s, wr_r, wc_s, wc_r, z_s, z_r,
                  gy_s, gy_r, gx_s, gx_r, gc_s, gc_r):
@@ -53,7 +53,6 @@
     mvs, ts, rts = (mv0, mv1), (t0, t1), (rt0, rt1)
     cols = (pl.ds(0, HALF), pl.ds(HALF, HALF))
     local = [
-        pltpu.make_async_copy(w_ref.at[x], wg.at[x, y, c], loc.at[0]),
         pltpu.make_async_copy(a_ref, ag.at[x], loc.at[1]),
         pltpu.make_async_copy(lat_ref, lat, loc.at[2]),
         pltpu.make_async_copy(res_ref, res, loc.at[3]),
@@ -74,6 +73,11 @@
     def _(k):
         pl.semaphore_signal(barrier, inc=1, device_id=((z + k) % 8, s, h), device_id_type=MESH)
 
+    for n in range(2):
+        rows = raw_ref[:, n, :]
+        for k in range(4):
+            w_ref[k, :, n * 384:(n + 1) * 384] = rows[:, k * 384:(k + 1) * 384]
+    wg[x, y, c] = w_ref[x]
     pl.semaphore_wait(barrier, 38)
 
     def ring(me, at, lo, hi, to, ss, rs):
@@ -154,136 +158,177 @@
     pos = ((((r // 16) % 4) * 4 + r // 128) * 2 + (r // 64) % 2) * 16 + r % 16
     bias = jnp.where(pos < len_ref[assign_ref[z]], 0.0, -1e9)
 
-    def cross(b):
-        for j in range(3):
-            at = lanes(b * 3 + j)
-            k = g[b, :, :, :, j * HDIM:(j + 1) * HDIM].reshape(512, HDIM)
-            v = g[b, :, :, :, 384 + j * HDIM:384 + (j + 1) * HDIM].reshape(512, HDIM)
+    parts, gots, gs = (part0, part1), (got0, got1), (g0, g1)
+    group_heads = ((0, 1), (2,))
+
+    def cross(b, n):
+        heads = group_heads[n]
+        for j, head in enumerate(heads):
+            at = lanes(b * 3 + head)
+            vj = len(heads) + j
+            k = gs[n][b, :, :, :, j * HDIM:(j + 1) * HDIM].reshape(512, HDIM)
+            v = gs[n][b, :, :, :, vj * HDIM:(vj + 1) * HDIM].reshape(512, HDIM)
             w = soft(qk(cq[:, at], k) + bias)
             acc[:, at] = acc[:, at] + jnp.dot(w, v, preferred_element_type=jnp.float32)
 
-    wx = []
-    for k in (1, 2, 3):
-        to = (x + k) % 4
-        d = put(w_ref.at[to], wg.at[x, y, c], wx_s.at[k - 1], wx_r.at[k - 1], dev(z, to, y, c))
-        d.start()
-        wx.append(d)
-    local[1].wait()
+    wx = [put(w_ref.at[(x + k) % 4], wg.at[x, y, c], wx_s.at[k - 1], wx_r.at[k - 1],
+              dev(z, (x + k) % 4, y, c)) for k in (1, 2, 3)]
+    wx_in = [put(w_ref.at[x], wg.at[(x + 4 - k) % 4, y, c], wx_s.at[k - 1], wx_r.at[k - 1],
+                 dev(z, (x + 4 - k) % 4, y, c)) for k in (1, 2, 3)]
     a_start, a_forward, a_finish, a_drain = ring(
         x, lambda k: ag.at[k], lambda k: ag.at[k, 0:4], lambda k: ag.at[k, 4:8],
         lambda k: dev(z, k, y, c), ar_s, ar_r)
-    a_start()
-    exchange(0, 1, 8)
-    local[0].wait()
-    for k in (1, 2, 3):
-        frm = (x + 4 - k) % 4
-        put(w_ref.at[x], wg.at[frm, y, c], wx_s.at[k - 1], wx_r.at[k - 1],
-            dev(z, frm, y, c)).wait_recv()
     w_start, w_forward, w_finish, w_drain = ring(
         y, lambda k: wg.at[:, k, c], lambda k: wg.at[0:2, k, c], lambda k: wg.at[2:4, k, c],
         lambda k: dev(z, x, k, c), wr_s, wr_r)
-    w_start()
+    swap = put(wg.at[:, :, c], wg.at[:, :, c], wc_s, wc_r, dev(z, x, y, 1 - c))
+    swap_in = put(wg.at[:, :, 1 - c], wg.at[:, :, 1 - c], wc_s, wc_r, dev(z, x, y, 1 - c))
+    far = (4, 3, 5, 2, 6, 1, 7)
+    sent = [[put(parts[n].at[(z + k) % 8], gots[n].at[k - 1], z_s.at[n, k - 1], z_r.at[n, k - 1],
+                 dev((z + k) % 8, x, y, c)) for k in far] for n in range(2)]
+    blocks = [(x + k) % 4 for k in (0, 3, 1, 2)]
+
+    def gather_y(n):
+        g = gs[n]
+        return ring(y, lambda k: g.at[x, k, c], lambda k: g.at[x, k, c, 0:32],
+                    lambda k: g.at[x, k, c, 32:64], lambda k: dev(z, x, k, c),
+                    gy_s.at[n], gy_r.at[n])
+
+    def gather_x(n):
+        g = gs[n]
+        return ring(x, lambda k: g.at[k, :, c], lambda k: g.at[k, 0:2, c],
+                    lambda k: g.at[k, 2:4, c], lambda k: dev(z, k, y, c), gx_s.at[n], gx_r.at[n])
+
+    ry, rx = [gather_y(n) for n in range(2)], [gather_x(n) for n in range(2)]
+    swaps = [[put(gs[n].at[b, :, c], gs[n].at[b, :, c], gc_s.at[n, i], gc_r.at[n, i],
+                  dev(z, x, y, 1 - c)) for i, b in enumerate(blocks)] for n in range(2)]
+    swapped = [[put(gs[n].at[b, :, 1 - c], gs[n].at[b, :, 1 - c], gc_s.at[n, i], gc_r.at[n, i],
+                    dev(z, x, y, 1 - c)) for i, b in enumerate(blocks)] for n in range(2)]
+
+    def weights_x():
+        for d in wx:
+            d.start()
+        local[0].wait()
+        a_start()
+
+    def weights_y():
+        for d in wx_in:
+            d.wait_recv()
+        w_start()
+
+    def weights_core():
+        w_finish()
+        swap.start()
+        a_finish()
+
+    def product():
+        swap_in.wait_recv()
+        for n, (width, k0) in enumerate(((256, 0), (128, 256))):
+            rhs = jnp.concatenate([wg[:, :, :, :, k0:k0 + width],
+                                   wg[:, :, :, :, 384 + k0:384 + k0 + width]],
+                                  axis=-1).reshape(FEAT, 2 * width)
+            for half in range(2):
+                lhs = jnp.concatenate(
+                    [ag[xb, assign_ref[half * 4 + j]] for j in range(4) for xb in range(4)], axis=0)
+                prod = jnp.dot(lhs, rhs, preferred_element_type=jnp.float32)
+                parts[n][half * 4:half * 4 + 4] = prod.astype(jnp.bfloat16).reshape(4, 64, 2 * width)
+            for d in sent[n]:
+                d.start()
+
+    def reduce_z(n):
+        total = parts[n][z].astype(jnp.float32)
+        for k in range(1, 8):
+            put(parts[n].at[0], gots[n].at[k - 1], z_s.at[n, k - 1], z_r.at[n, k - 1],
+                dev((z + 8 - k) % 8, x, y, c)).wait_recv()
+            total = total + gots[n][k - 1].astype(jnp.float32)
+        gs[n][x, y, c] = total.astype(jnp.bfloat16)
+        ry[n][0]()
+
+    def pairs_x(n):
+        ry[n][2]()
+        rx[n][0]()
+        swaps[n][0].start()
+
+    def pairs_xf(n):
+        rx[n][1]()
+        swaps[n][1].start()
+        swaps[n][2].start()
+
+    def pairs_xl(n):
+        rx[n][2]()
+        swaps[n][3].start()
+
+    def cross_block(n, i):
+        swapped[n][i].wait_recv()
+        cross(blocks[i], n)
+
+    def take(half):
+        all_of(mvs[half], ex_s, ex_r, half).wait_recv()
+        local[3 + half].wait()
+        temporal(half)
+
+    def finish(half):
+        all_of(rts[half], rt_s, rt_r, half).wait_recv()
+        back = rts[half][...].reshape(256, HALF).astype(jnp.float32)
+        out_ref[:, cols[half]] = (acc[:, cols[half]] + back).astype(jnp.bfloat16)
+
+    weights_x()
+    exchange(0, 1, 8)
+    weights_y()
     exchange(0, 8, 16)
+    local[1].wait()
     local[2].wait()
-    local[3].wait()
     spatial(0, 2)
     a_forward()
     w_forward()
     exchange(0, 16, 32)
+    spatial(2, 6)
+    weights_core()
+    product()
+    exchange(1, 8, 24)
+    take(0)
+    reduce_z(0)
+    reduce_z(1)
+    exchange(1, 24, 32)
+    ry[0][1]()
+    ry[1][1]()
+    pairs_x(0)
     exchange(1, 1, 8)
-    spatial(2, 6)
-    a_finish()
-    w_finish()
-    swap = put(wg.at[:, :, c], wg.at[:, :, c], wc_s, wc_r, dev(z, x, y, 1 - c))
-    swap.start()
-    put(wg.at[:, :, 1 - c], wg.at[:, :, 1 - c], wc_s, wc_r, dev(z, x, y, 1 - c)).wait_recv()
-
-    for half in range(2):
-        lhs = jnp.concatenate(
-            [ag[xb, assign_ref[half * 4 + j]] for j in range(4) for xb in range(4)], axis=0)
-        prod = jnp.dot(lhs, wg[...].reshape(FEAT, CB), preferred_element_type=jnp.float32)
-        part[half * 4:half * 4 + 4] = prod.astype(jnp.bfloat16).reshape(4, 64, CB)
-    sent = []
-    for k in (4, 3, 5, 2, 6, 1, 7):
-        to = (z + k) % 8
-        d = put(part.at[to], got.at[k - 1], z_s.at[k - 1], z_r.at[k - 1], dev(to, x, y, c))
-        d.start()
-        sent.append(d)
-
-    exchange(1, 8, 20)
-    all_of(mv0, ex_s, ex_r, 0).wait_recv()
-    local[4].wait()
-    temporal(0)
-
-    total = part[z].astype(jnp.float32)
-    for k in range(1, 8):
-        frm = (z + 8 - k) % 8
-        put(part.at[0], got.at[k - 1], z_s.at[k - 1], z_r.at[k - 1], dev(frm, x, y, c)).wait_recv()
-        total = total + got[k - 1].astype(jnp.float32)
-    g[x, y, c] = total.astype(jnp.bfloat16)
-
-    y_start, y_forward, y_finish, y_drain = ring(
-        y, lambda k: g.at[x, k, c], lambda k: g.at[x, k, c, 0:32],
-        lambda k: g.at[x, k, c, 32:64], lambda k: dev(z, x, k, c), gy_s, gy_r)
-    x_start, x_forward, x_finish, x_drain = ring(
-        x, lambda k: g.at[k, :, c], lambda k: g.at[k, 0:2, c],
-        lambda k: g.at[k, 2:4, c], lambda k: dev(z, k, y, c), gx_s, gx_r)
-    blocks = [(x + k) % 4 for k in (0, 3, 1, 2)]
-    swaps = [put(g.at[b, :, c], g.at[b, :, c], gc_s.at[i], gc_r.at[i], dev(z, x, y, 1 - c))
-             for i, b in enumerate(blocks)]
-    swapped = [put(g.at[b, :, 1 - c], g.at[b, :, 1 - c], gc_s.at[i], gc_r.at[i],
-                   dev(z, x, y, 1 - c)) for i, b in enumerate(blocks)]
-    y_start()
-    exchange(1, 20, 32)
-    y_forward()
+    local[5].wait()
+    cross_block(0, 0)
+    pairs_x(1)
+    cross_block(1, 0)
+    pairs_xf(0)
     give_back(0)
-    y_finish()
-    x_start()
-    swaps[0].start()
-    local[6].wait()
-    swapped[0].wait_recv()
-    cross(blocks[0])
-
-    all_of(mv1, ex_s, ex_r, 1).wait_recv()
-    local[5].wait()
-    temporal(1)
+    cross_block(0, 1)
+    cross_block(0, 2)
+    pairs_xf(1)
+    take(1)
     give_back(1)
-
-    x_forward()
-    swaps[1].start()
-    swaps[2].start()
-    swapped[1].wait_recv()
-    cross(blocks[1])
-    swapped[2].wait_recv()
-    cross(blocks[2])
-    x_finish()
-    swaps[3].start()
-    swapped[3].wait_recv()
-    cross(blocks[3])
-
-    for half in range(2):
-        all_of(rts[half], rt_s, rt_r, half).wait_recv()
-        back = rts[half][...].reshape(256, HALF).astype(jnp.float32)
-        out_ref[:, cols[half]] = (acc[:, cols[half]] + back).astype(jnp.bfloat16)
+    cross_block(1, 1)
+    cross_block(1, 2)
+    pairs_xl(0)
+    cross_block(0, 3)
+    pairs_xl(1)
+    cross_block(1, 3)
+    finish(0)
+    finish(1)
 
     for half in range(2):
         all_of(mvs[half], ex_s, ex_r, half).wait_send()
         all_of(ts[half], rt_s, rt_r, half).wait_send()
-    for d in wx + [swap] + sent + swaps:
+    for d in wx + [swap] + sent[0] + sent[1] + swaps[0] + swaps[1]:
         d.wait_send()
-    a_drain()
-    w_drain()
-    y_drain()
-    x_drain()
+    for drain in (a_drain, w_drain, ry[0][3], ry[1][3], rx[0][3], rx[1][3]):
+        drain()
 
 
 def body(latent_qkv, cross_query, residual, prompt_states, kv_weight, prompt_lengths, assignment):
     latent = jnp.transpose(latent_qkv[0, 0], (1, 0, 2)).reshape(3, 32, 8, 1536)
-    weight = jnp.transpose(kv_weight.reshape(ROWS, 2, 4, 384), (2, 0, 1, 3)).reshape(4, ROWS, CB)
     sem = pltpu.SemaphoreType.DMA
     vm = pl.BlockSpec(memory_space=pltpu.VMEM)
     sm = pl.BlockSpec(memory_space=pltpu.SMEM)
-    hb = pl.BlockSpec(memory_space=pl.ANY)
+    hb = pl.BlockSpec(memory_space=pltpu.MemorySpace.HBM)
     b16, f32 = jnp.bfloat16, jnp.float32
     out = pl.pallas_call(
         block_kernel,
@@ -291,6 +336,7 @@
         in_specs=[sm, sm, hb, hb, hb, vm, vm],
         out_specs=vm,
         scratch_shapes=[
+            pltpu.VMEM((4, ROWS, CB), b16),
             pltpu.VMEM((3, 32, 8, 1536), b16),
             pltpu.VMEM((256, 1536), b16),
             pltpu.VMEM((256, 1536), b16),
@@ -300,17 +346,18 @@
             pltpu.VMEM((32, 8, HALF), b16), pltpu.VMEM((32, 8, HALF), b16),
             pltpu.VMEM((4, 8, ROWS, FEAT), b16),
             pltpu.VMEM((4, 4, 2, ROWS, CB), b16),
-            pltpu.VMEM((8, 64, CB), b16),
-            pltpu.VMEM((7, 64, CB), b16),
-            pltpu.VMEM((4, 4, 2, 64, CB), b16),
+            pltpu.VMEM((8, 64, 512), b16), pltpu.VMEM((8, 64, 256), b16),
+            pltpu.VMEM((7, 64, 512), b16), pltpu.VMEM((7, 64, 256), b16),
+            pltpu.VMEM((4, 4, 2, 64, 512), b16), pltpu.VMEM((4, 4, 2, 64, 256), b16),
             sem((7,)), sem((2,)), sem((2,)), sem((2,)), sem((2,)),
             sem((3,)), sem((3,)), sem((4,)), sem((4,)), sem((4,)), sem((4,)),
-            sem, sem, sem((7,)), sem((7,)),
-            sem((4,)), sem((4,)), sem((4,)), sem((4,)), sem((4,)), sem((4,)),
+            sem, sem, sem((2, 7)), sem((2, 7)),
+            sem((2, 4)), sem((2, 4)), sem((2, 4)), sem((2, 4)), sem((2, 4)), sem((2, 4)),
         ],
-        compiler_params=pltpu.CompilerParams(collective_id=0, has_side_effects=True),
+        compiler_params=pltpu.CompilerParams(
+            collective_id=0, has_side_effects=True),
         name="block",
-    )(assignment, prompt_lengths, latent, cross_query[0, 0], residual[0, 0], prompt_states, weight)
+    )(assignment, prompt_lengths, latent, cross_query[0, 0], residual[0, 0], prompt_states, kv_weight)
     return out[None, None]
 
 

time: 119 us -> 109 us (0.916)
  Pallas kernels: 115 us -> 107 us
  local copies, waits for them, and re-layouts: 3.73 us -> 2.06 us
    pallas_call x1, Pallas kernels: 115 us -> 107 us  [body(): pl.pallas_call(block_kernel, out_shape=jax.ShapeDtypeStruct((256, 1536),...]
    reshape x2 -> x0, local copies, waits for them, and re-layouts: 1.67 us -> none  [the longest x1 0.96 us: body(): kv_weight.reshape(ROWS, 2, 4, 384)]
where the time goes in v3:
time: 109 us
  Pallas kernels  107 us (98%)
  local copies, waits for them, and re-layouts  2.06 us (2%)
    pallas_call x1, Pallas kernels, body(): pl.pallas_call(block_kernel, out_shape=jax.ShapeDtypeStruct((256, 1536),...  107 us

profile of v3, /device:TPU:1, one launch (start us, length us, event | category | flops | bytes accessed | tf_op | source)
XLA Modules:
  0.0 108.8 jit_solution(18379709475921129459)
XLA Ops:
  0.0 106.8 %block.1 = bf16[256,1536]{1,0:T(8,128)(2,1)} custom-call(s32[8]{0:T(128)} %assign_ref.1, s32[8]{0:T(128)} %len_ref.1, bf16[3,32,8,1536]{3,2,1,0:T(8,128)(2,1)} %bitcast.9, bf16[256,1536]{1,0:T(8,128)(2,1)} %bitcast.10, bf16[256,1536]{1,0:T(8,128)(2,1)} %bitcast.11, bf16[8,16,512]{2,1,0:T(8,128)(2,1)} %a_ref.1, bf16[16,2,1536]{2,1,0:T(2,128)(2,1)} %raw_ref.1), custom_call_target="tpu_custom_call" | custom-call | tf_op jit(solution)/shard_map/block/pallas_call | solution.py:333
  106.8 2.1 %copy.9 = bf16[1,1,256,1536]{3,2,1,0:T(8,128)(2,1)} copy(bf16[1,1,256,1536]{3,2,1,0:T(8,128)(2,1)} %bitcast.8) | data formatting | bytes 1572864

commit v4 on v3

--- a/solution.py
+++ b/solution.py
@@ -119,8 +119,8 @@
             put(lat_ref.at[:, to, :, cols[half]], mvs[half].at[s],
                 ex_s.at[half], ex_r.at[half], (z, to, h)).start()
 
-    def give_back(half):
-        @pl.loop(1, 32)
+    def give_back(half, lo=1, hi=32):
+        @pl.loop(lo, hi)
         def _(t):
             to = peer(t)
             put(ts[half].at[to], rts[half].at[s], rt_s.at[half], rt_r.at[half], (z, to, h)).start()
@@ -273,15 +273,15 @@
         out_ref[:, cols[half]] = (acc[:, cols[half]] + back).astype(jnp.bfloat16)
 
     weights_x()
-    exchange(0, 1, 8)
+    exchange(0, 1, 4)
     weights_y()
-    exchange(0, 8, 16)
+    exchange(0, 4, 12)
     local[1].wait()
     local[2].wait()
     spatial(0, 2)
     a_forward()
     w_forward()
-    exchange(0, 16, 32)
+    exchange(0, 12, 32)
     spatial(2, 6)
     weights_core()
     product()
@@ -298,8 +298,9 @@
     cross_block(0, 0)
     pairs_x(1)
     cross_block(1, 0)
+    give_back(0, 1, 8)
     pairs_xf(0)
-    give_back(0)
+    give_back(0, 8, 32)
     cross_block(0, 1)
     cross_block(0, 2)
     pairs_xf(1)

time: 109 us -> 107 us (0.982)
  the two profiles are of different devices: /device:TPU:1 before, /device:TPU:9 now
where the time goes in v4:
time: 107 us
  Pallas kernels  105 us (98%)
  local copies, waits for them, and re-layouts  2.06 us (2%)
    pallas_call x1, Pallas kernels, body(): pl.pallas_call(block_kernel, out_shape=jax.ShapeDtypeStruct((256, 1536),...  105 us

profile of v4, /device:TPU:9, one launch (start us, length us, event | category | flops | bytes accessed | tf_op | source)
XLA Modules:
  0.0 106.6 jit_solution(12411483299037022706)
XLA Ops:
  0.0 104.6 %block.1 = bf16[256,1536]{1,0:T(8,128)(2,1)} custom-call(s32[8]{0:T(128)} %assign_ref.1, s32[8]{0:T(128)} %len_ref.1, bf16[3,32,8,1536]{3,2,1,0:T(8,128)(2,1)} %bitcast.9, bf16[256,1536]{1,0:T(8,128)(2,1)} %bitcast.10, bf16[256,1536]{1,0:T(8,128)(2,1)} %bitcast.11, bf16[8,16,512]{2,1,0:T(8,128)(2,1)} %a_ref.1, bf16[16,2,1536]{2,1,0:T(2,128)(2,1)} %raw_ref.1), custom_call_target="tpu_custom_call" | custom-call | tf_op jit(solution)/shard_map/block/pallas_call | solution.py:334
  104.6 2.1 %copy.9 = bf16[1,1,256,1536]{3,2,1,0:T(8,128)(2,1)} copy(bf16[1,1,256,1536]{3,2,1,0:T(8,128)(2,1)} %bitcast.8) | data formatting | bytes 1572864
